TPU v7x, 32 devices: a whole 2x2x4 slice. The times are simulated.
32 devices in a mesh: head: 4 (over z), outer: 2 (over core), inner: 4 (over y, x).
Axes of the slice: x: 2, y: 2, z: 4, core: 2. Of those that a mesh axis runs over, the one named last changes fastest.
Arguments:
- query: bfloat16 [4096, 8192], P(('outer', 'inner', 'head')), may hold values from -100 to 100
- keys: bfloat16 [4096, 1024], P(('outer', 'inner', 'head')), may hold values from -4.5 to 4.5
- values: bfloat16 [4096, 1024], P(('outer', 'inner', 'head')), may hold values from -6 to 6
- lengths: int32 [8], replicated, may hold values from 1 to 1024, 4096 in all
Outputs:
- attended: bfloat16 [4096, 8192], P(('outer', 'inner', 'head'))
Inputs may be any that keep to these rules, and one draw needn't show every extreme that they name: `lengths`: they sum to 4096, and the longest is exactly 1024.
All inputs are finite; a program needn't handle non-finite values.
Results may differ from a plain program's by a relative error of at most 0.0038.
Values may be sent and summed in bfloat16 or wider, within the bound.
A program may use at most 64 MiB of HBM per device.

v0:
```python
import math
import jax
import jax.numpy as jnp
from jax import lax
from jax.sharding import PartitionSpec as P

HEAD_SIZE = 128


def from_behind(value, axis, steps):
    count = lax.axis_size(axis)
    leading, last = (max(0, -steps), min(count, count - steps))
    return lax.ppermute(value, axis, [(source, source + steps) for source in range(leading, last)])


def doc_numbers(lengths, start_pos, count):
    ends = jnp.cumsum(lengths)
    positions = start_pos + lax.iota(jnp.int32, count)
    numbers = jnp.sum((positions[:, None] >= ends[None, :]).astype(jnp.int32), axis=1)
    return (numbers, positions)


def per_device(query, keys, values, lengths):
    query_local, keys_local, values_local = (
        lax.all_to_all(query, "head", split_axis=1, concat_axis=0, tiled=True),
        lax.all_to_all(keys, "head", split_axis=1, concat_axis=0, tiled=True),
        lax.all_to_all(values, "head", split_axis=1, concat_axis=0, tiled=True),
    )
    local_len = query_local.shape[0]
    pair_heads = keys_local.shape[1] // HEAD_SIZE
    group_width = query_local.shape[1] // keys_local.shape[1]
    context_count = lax.axis_size(("outer", "inner"))
    reach_hops = min(2, context_count // 4)
    position_index = lax.axis_index(("outer", "inner"))
    query_docs, query_pos = doc_numbers(lengths, position_index * local_len, local_len)
    query_groups = jnp.transpose(
        query_local.reshape(local_len, pair_heads, group_width, HEAD_SIZE), (2, 0, 1, 3)
    )
    score_scale = 1.0 / math.sqrt(HEAD_SIZE)

    def attend(state, stacked, distance):
        key_heads = stacked[0].reshape(local_len, pair_heads, HEAD_SIZE)
        value_heads = stacked[1].reshape(local_len, pair_heads, HEAD_SIZE)
        key_docs, key_pos = doc_numbers(lengths, (position_index - distance) * local_len, local_len)
        visible = (
            (query_docs[:, None] == key_docs[None, :])
            & (key_pos[None, :] <= query_pos[:, None])
            & (key_pos[None, :] >= 0)
        )

        def one_group(operands):
            query_part, running_max, running_total, running_sum = operands
            scores = (
                jnp.einsum(
                    "qkd,ckd->kqc", query_part, key_heads, preferred_element_type=jnp.float32
                )
                * score_scale
            )
            masked = jnp.where(visible, scores, -1e30)
            new_max = jnp.maximum(running_max, jnp.max(masked, axis=2))
            weights = jnp.where(visible, jnp.exp(masked - new_max[..., None]), 0.0)
            shrink = jnp.exp(running_max - new_max)
            new_total = running_total * shrink + jnp.sum(weights, axis=2)
            update = jnp.einsum(
                "kqc,ckd->qkd",
                weights.astype(jnp.bfloat16),
                value_heads,
                preferred_element_type=jnp.float32,
            )
            new_sum = running_sum * jnp.transpose(shrink, (1, 0))[..., None] + update
            return (new_max, new_total, new_sum)

        return lax.map(one_group, (query_groups, state[0], state[1], state[2]))

    start_state = (
        jnp.full((group_width, pair_heads, local_len), -1e30, jnp.float32),
        jnp.zeros((group_width, pair_heads, local_len), jnp.float32),
        jnp.zeros((group_width, local_len, pair_heads, HEAD_SIZE), jnp.float32),
    )
    own_pair = jnp.stack((keys_local, values_local))
    state = attend(start_state, own_pair, 0)
    carried = own_pair
    for distance in range(1, reach_hops + 1):
        carried = from_behind(carried, ("outer", "inner"), 1)
        state = attend(state, carried, distance)
    running_max, running_total, running_sum = state
    outcome = running_sum / jnp.transpose(running_total, (0, 2, 1))[..., None]
    outcome = jnp.transpose(outcome, (1, 2, 0, 3))
    outcome = outcome.reshape(local_len, pair_heads * group_width * HEAD_SIZE).astype(jnp.bfloat16)
    return lax.all_to_all(outcome, "head", split_axis=0, concat_axis=1, tiled=True)


def solution(mesh):
    placed = (
        P(("outer", "inner", "head"), None),
        P(("outer", "inner", "head"), None),
        P(("outer", "inner", "head"), None),
        P(),
    )
    return jax.shard_map(
        per_device,
        mesh=mesh,
        in_specs=placed,
        out_specs=P(("outer", "inner", "head"), None),
        check_vma=False,
    )
```

profile of v0, /device:TPU:0, one launch (start us, length us, event | category | flops | bytes accessed | tf_op | source)
XLA Modules:
  0.0 246.9 jit_solution(3934203246122695590)
XLA Ops:
  0.0 1.9 copy.56
  1.9 6.3 %all-to-all-start.1 = ((bf16[128,4,256]{0,2,1:T(8,128)(2,1)}), bf16[128,4,256]{0,2,1:T(8,128)(2,1)S(1)}, u32[]{:S(2)}, u32[]{:S(2)}) async-start(bf16[128,4,256]{0,2,1:T(8,128)(2,1)} %bitcast.2), calls=%async_computation.1 | async-start | bytes 524288 | tf_op jit(solution)/shard_map/all_to_all | solution.py:26
  8.3 1.8 copy.58
  10.1 7.1 %all-to-all-done.1 = bf16[128,4,256]{0,2,1:T(8,128)(2,1)S(1)} async-done(((bf16[128,4,256]{0,2,1:T(8,128)(2,1)}), bf16[128,4,256]{0,2,1:T(8,128)(2,1)S(1)}, u32[]{:S(2)}, u32[]{:S(2)}) %all-to-all-start.1) | async-done | bytes 262176 | tf_op jit(solution)/shard_map/all_to_all | solution.py:26
  17.2 3.4 %all-to-all-start.2 = ((bf16[128,4,256]{0,2,1:T(8,128)(2,1)}), bf16[128,4,256]{0,2,1:T(8,128)(2,1)S(1)}, u32[]{:S(2)}, u32[]{:S(2)}) async-start(bf16[128,4,256]{0,2,1:T(8,128)(2,1)} %bitcast.4), calls=%async_computation.2 | async-start | bytes 524288 | tf_op jit(solution)/shard_map/all_to_all | solution.py:27
  22.2 5.4 %all-to-all-done.2 = bf16[128,4,256]{0,2,1:T(8,128)(2,1)S(1)} async-done(((bf16[128,4,256]{0,2,1:T(8,128)(2,1)}), bf16[128,4,256]{0,2,1:T(8,128)(2,1)S(1)}, u32[]{:S(2)}, u32[]{:S(2)}) %all-to-all-start.2) | async-done | bytes 262176 | tf_op jit(solution)/shard_map/all_to_all | solution.py:27
  27.6 3.6 %all-to-all-start = ((bf16[128,4,2048]{2,0,1:T(8,128)(2,1)}), bf16[128,4,2048]{2,0,1:T(8,128)(2,1)S(1)}, u32[]{:S(2)}, u32[]{:S(2)}) async-start(bf16[128,4,2048]{2,0,1:T(8,128)(2,1)} %bitcast.143), calls=%async_computation | async-start | bytes 4194304 | tf_op jit(solution)/shard_map/all_to_all | solution.py:25
  31.6 4.2 %collective-permute-start = (bf16[2,512,256]{2,1,0:T(8,128)(2,1)S(1)}, bf16[2,512,256]{2,1,0:T(8,128)(2,1)}, u32[]{:S(2)}, u32[]{:S(2)}) collective-permute-start(bf16[2,512,256]{2,1,0:T(8,128)(2,1)S(1)} %pad_maximum_fusion), channel_id=1, source_target_pairs={{0,1},{1,2},{2,3},{3,4},{4,5},{5,6},{6,7},{8,9},{9,10},{10,11},{11... | collective-permute-start | bytes 1572872 | tf_op jit(solution)/shard_map/ppermute | solution.py:13
  35.8 7.3 %collective-permute-done = bf16[2,512,256]{2,1,0:T(8,128)(2,1)} collective-permute-done((bf16[2,512,256]{2,1,0:T(8,128)(2,1)S(1)}, bf16[2,512,256]{2,1,0:T(8,128)(2,1)}, u32[]{:S(2)}, u32[]{:S(2)}) %collective-permute-start) | collective-permute-done | bytes 524320 | tf_op jit(solution)/shard_map/ppermute | solution.py:13
  43.2 5.3 %collective-permute-start.1 = (bf16[2,512,256]{2,1,0:T(8,128)(2,1)}, bf16[2,512,256]{2,1,0:T(8,128)(2,1)}, u32[]{:S(2)}, u32[]{:S(2)}) collective-permute-start(bf16[2,512,256]{2,1,0:T(8,128)(2,1)} %collective-permute-done), channel_id=1, source_target_pairs={{0,1},{1,2},{2,3},{3,4},{4,5},{5,6},{6,7},{8,9},{9,10},{10,11},{11... | collective-permute-start | bytes 1572872 | tf_op jit(solution)/shard_map/ppermute | solution.py:13
  52.1 5.0 %collective-permute-done.1 = bf16[2,512,256]{2,1,0:T(8,128)(2,1)} collective-permute-done((bf16[2,512,256]{2,1,0:T(8,128)(2,1)}, bf16[2,512,256]{2,1,0:T(8,128)(2,1)}, u32[]{:S(2)}, u32[]{:S(2)}) %collective-permute-start.1) | collective-permute-done | bytes 524320 | tf_op jit(solution)/shard_map/ppermute | solution.py:13
  58.8 17.9 %all-to-all-done = bf16[128,4,2048]{2,0,1:T(8,128)(2,1)S(1)} async-done(((bf16[128,4,2048]{2,0,1:T(8,128)(2,1)}), bf16[128,4,2048]{2,0,1:T(8,128)(2,1)S(1)}, u32[]{:S(2)}, u32[]{:S(2)}) %all-to-all-start) | async-done | bytes 2097184 | tf_op jit(solution)/shard_map/all_to_all | solution.py:25
  77.8 2.4 broadcast.125.clone.1
  80.3 27.0 %while.43 = (s32[]{:T(128)}, f32[8,2,512]{2,1,0:T(2,128)S(1)}, f32[8,2,512]{2,1,0:T(2,128)S(1)}, f32[8,512,2,128]{3,1,2,0:T(8,128)}, bf16[8,512,2,128]{3,1,2,0:T...) while((s32[]{:T(128)}, f32[8,2,512]{2,1,0:T(2,128)S(1)}, ...), condition=%wide.region_5.6_spmd.clone, body=%wide.region_2.0_spmd.clone.sunk | while | flops 276435968 | bytes 9753745 | solution.py:73
  81.4 1.8 fusion.111
  84.7 1.8 fusion.111
  88.1 1.8 fusion.111
  91.5 1.8 fusion.111
  94.8 1.8 fusion.111
  98.2 1.8 fusion.111
  101.5 1.8 fusion.111
  104.8 1.8 fusion.111
  107.2 2.4 broadcast.125.clone
  109.6 34.8 %while.44 = (s32[]{:T(128)}, f32[8,2,512]{2,1,0:T(2,128)S(1)}, f32[8,2,512]{2,1,0:T(2,128)S(1)}, f32[8,512,2,128]{3,1,2,0:T(8,128)}, f32[8,2,512]{2,1,0:T(2,128)...) while((s32[]{:T(128)}, f32[8,2,512]{2,1,0:T(2,128)S(1)}, ...), condition=%wide.region_10.11_spmd.clone, body=%wide.region_7.10_spmd.clone.sunk | while | flops 276566016 | bytes 9245857 | solution.py:73
  110.6 2.8 %fusion.119 = f32[8,512,2,128]{3,1,2,0:T(8,128)} fusion(f32[8,512,2,128]{3,1,2,0:T(8,128)} %get-tuple-element.807, s32[]{:T(128)} %get-tuple-element.804, bf16[512,2,128]{2,0,1:T(8,128)(2,1)S(1)} %get-tuple-element.829, f32[2,512,512]{1,2,0:T(8,128)S(1)} %get-tuple-element.731, f32[2,512]{1,0:T(2,128)S(1)} %get-tuple-element.733, ...), kind=kOutput, calls=%fused_computation.40.clone.1 | convolution fusion | flops 137101312 | bytes 3678720 | tf_op jit(solution)/shard_map/while/body/eval_jaxpr/kqc,ckd->qkd/dot_general | solution.py:64
  114.9 2.8 %fusion.119 = f32[8,512,2,128]{3,1,2,0:T(8,128)} fusion(f32[8,512,2,128]{3,1,2,0:T(8,128)} %get-tuple-element.807, s32[]{:T(128)} %get-tuple-element.804, bf16[512,2,128]{2,0,1:T(8,128)(2,1)S(1)} %get-tuple-element.829, f32[2,512,512]{1,2,0:T(8,128)S(1)} %get-tuple-element.731, f32[2,512]{1,0:T(2,128)S(1)} %get-tuple-element.733, ...), kind=kOutput, calls=%fused_computation.40.clone.1 | convolution fusion | flops 137101312 | bytes 3678720 | tf_op jit(solution)/shard_map/while/body/eval_jaxpr/kqc,ckd->qkd/dot_general | solution.py:64
  119.2 2.8 %fusion.119 = f32[8,512,2,128]{3,1,2,0:T(8,128)} fusion(f32[8,512,2,128]{3,1,2,0:T(8,128)} %get-tuple-element.807, s32[]{:T(128)} %get-tuple-element.804, bf16[512,2,128]{2,0,1:T(8,128)(2,1)S(1)} %get-tuple-element.829, f32[2,512,512]{1,2,0:T(8,128)S(1)} %get-tuple-element.731, f32[2,512]{1,0:T(2,128)S(1)} %get-tuple-element.733, ...), kind=kOutput, calls=%fused_computation.40.clone.1 | convolution fusion | flops 137101312 | bytes 3678720 | tf_op jit(solution)/shard_map/while/body/eval_jaxpr/kqc,ckd->qkd/dot_general | solution.py:64
  123.6 2.8 %fusion.119 = f32[8,512,2,128]{3,1,2,0:T(8,128)} fusion(f32[8,512,2,128]{3,1,2,0:T(8,128)} %get-tuple-element.807, s32[]{:T(128)} %get-tuple-element.804, bf16[512,2,128]{2,0,1:T(8,128)(2,1)S(1)} %get-tuple-element.829, f32[2,512,512]{1,2,0:T(8,128)S(1)} %get-tuple-element.731, f32[2,512]{1,0:T(2,128)S(1)} %get-tuple-element.733, ...), kind=kOutput, calls=%fused_computation.40.clone.1 | convolution fusion | flops 137101312 | bytes 3678720 | tf_op jit(solution)/shard_map/while/body/eval_jaxpr/kqc,ckd->qkd/dot_general | solution.py:64
  128.0 2.8 %fusion.119 = f32[8,512,2,128]{3,1,2,0:T(8,128)} fusion(f32[8,512,2,128]{3,1,2,0:T(8,128)} %get-tuple-element.807, s32[]{:T(128)} %get-tuple-element.804, bf16[512,2,128]{2,0,1:T(8,128)(2,1)S(1)} %get-tuple-element.829, f32[2,512,512]{1,2,0:T(8,128)S(1)} %get-tuple-element.731, f32[2,512]{1,0:T(2,128)S(1)} %get-tuple-element.733, ...), kind=kOutput, calls=%fused_computation.40.clone.1 | convolution fusion | flops 137101312 | bytes 3678720 | tf_op jit(solution)/shard_map/while/body/eval_jaxpr/kqc,ckd->qkd/dot_general | solution.py:64
  132.3 2.8 %fusion.119 = f32[8,512,2,128]{3,1,2,0:T(8,128)} fusion(f32[8,512,2,128]{3,1,2,0:T(8,128)} %get-tuple-element.807, s32[]{:T(128)} %get-tuple-element.804, bf16[512,2,128]{2,0,1:T(8,128)(2,1)S(1)} %get-tuple-element.829, f32[2,512,512]{1,2,0:T(8,128)S(1)} %get-tuple-element.731, f32[2,512]{1,0:T(2,128)S(1)} %get-tuple-element.733, ...), kind=kOutput, calls=%fused_computation.40.clone.1 | convolution fusion | flops 137101312 | bytes 3678720 | tf_op jit(solution)/shard_map/while/body/eval_jaxpr/kqc,ckd->qkd/dot_general | solution.py:64
  136.6 2.8 %fusion.119 = f32[8,512,2,128]{3,1,2,0:T(8,128)} fusion(f32[8,512,2,128]{3,1,2,0:T(8,128)} %get-tuple-element.807, s32[]{:T(128)} %get-tuple-element.804, bf16[512,2,128]{2,0,1:T(8,128)(2,1)S(1)} %get-tuple-element.829, f32[2,512,512]{1,2,0:T(8,128)S(1)} %get-tuple-element.731, f32[2,512]{1,0:T(2,128)S(1)} %get-tuple-element.733, ...), kind=kOutput, calls=%fused_computation.40.clone.1 | convolution fusion | flops 137101312 | bytes 3678720 | tf_op jit(solution)/shard_map/while/body/eval_jaxpr/kqc,ckd->qkd/dot_general | solution.py:64
  141.0 2.8 %fusion.119 = f32[8,512,2,128]{3,1,2,0:T(8,128)} fusion(f32[8,512,2,128]{3,1,2,0:T(8,128)} %get-tuple-element.807, s32[]{:T(128)} %get-tuple-element.804, bf16[512,2,128]{2,0,1:T(8,128)(2,1)S(1)} %get-tuple-element.829, f32[2,512,512]{1,2,0:T(8,128)S(1)} %get-tuple-element.731, f32[2,512]{1,0:T(2,128)S(1)} %get-tuple-element.733, ...), kind=kOutput, calls=%fused_computation.40.clone.1 | convolution fusion | flops 137101312 | bytes 3678720 | tf_op jit(solution)/shard_map/while/body/eval_jaxpr/kqc,ckd->qkd/dot_general | solution.py:64
  144.4 2.4 broadcast.125
  146.8 34.8 %while.45 = (s32[]{:T(128)}, f32[8,2,512]{2,1,0:T(2,128)S(1)}, f32[8,512,2,128]{3,1,2,0:T(8,128)}, f32[8,2,512]{2,1,0:T(2,128)S(1)}, f32[8,2,512]{2,1,0:T(2,128)...) while((s32[]{:T(128)}, f32[8,2,512]{2,1,0:T(2,128)S(1)}, ...), condition=%wide.region_15.16_spmd.clone, body=%wide.region_12.15_spmd.clone.sunk | while | flops 276566016 | bytes 9241753 | solution.py:73
  147.8 2.8 %fusion.127 = f32[8,512,2,128]{3,1,2,0:T(8,128)} fusion(f32[8,512,2,128]{3,1,2,0:T(8,128)} %get-tuple-element.853, s32[]{:T(128)} %get-tuple-element.851, bf16[512,2,128]{2,0,1:T(8,128)(2,1)S(1)} %get-tuple-element.874, f32[2,512,512]{1,2,0:T(8,128)S(1)} %get-tuple-element.751, f32[2,512]{1,0:T(2,128)S(1)} %get-tuple-element.753, ...), kind=kOutput, calls=%fused_computation.71.clone.1 | convolution fusion | flops 137101312 | bytes 3678720 | tf_op jit(solution)/shard_map/while/body/eval_jaxpr/kqc,ckd->qkd/dot_general | solution.py:64
  152.1 2.8 %fusion.127 = f32[8,512,2,128]{3,1,2,0:T(8,128)} fusion(f32[8,512,2,128]{3,1,2,0:T(8,128)} %get-tuple-element.853, s32[]{:T(128)} %get-tuple-element.851, bf16[512,2,128]{2,0,1:T(8,128)(2,1)S(1)} %get-tuple-element.874, f32[2,512,512]{1,2,0:T(8,128)S(1)} %get-tuple-element.751, f32[2,512]{1,0:T(2,128)S(1)} %get-tuple-element.753, ...), kind=kOutput, calls=%fused_computation.71.clone.1 | convolution fusion | flops 137101312 | bytes 3678720 | tf_op jit(solution)/shard_map/while/body/eval_jaxpr/kqc,ckd->qkd/dot_general | solution.py:64
  156.4 2.8 %fusion.127 = f32[8,512,2,128]{3,1,2,0:T(8,128)} fusion(f32[8,512,2,128]{3,1,2,0:T(8,128)} %get-tuple-element.853, s32[]{:T(128)} %get-tuple-element.851, bf16[512,2,128]{2,0,1:T(8,128)(2,1)S(1)} %get-tuple-element.874, f32[2,512,512]{1,2,0:T(8,128)S(1)} %get-tuple-element.751, f32[2,512]{1,0:T(2,128)S(1)} %get-tuple-element.753, ...), kind=kOutput, calls=%fused_computation.71.clone.1 | convolution fusion | flops 137101312 | bytes 3678720 | tf_op jit(solution)/shard_map/while/body/eval_jaxpr/kqc,ckd->qkd/dot_general | solution.py:64
  160.8 2.8 %fusion.127 = f32[8,512,2,128]{3,1,2,0:T(8,128)} fusion(f32[8,512,2,128]{3,1,2,0:T(8,128)} %get-tuple-element.853, s32[]{:T(128)} %get-tuple-element.851, bf16[512,2,128]{2,0,1:T(8,128)(2,1)S(1)} %get-tuple-element.874, f32[2,512,512]{1,2,0:T(8,128)S(1)} %get-tuple-element.751, f32[2,512]{1,0:T(2,128)S(1)} %get-tuple-element.753, ...), kind=kOutput, calls=%fused_computation.71.clone.1 | convolution fusion | flops 137101312 | bytes 3678720 | tf_op jit(solution)/shard_map/while/body/eval_jaxpr/kqc,ckd->qkd/dot_general | solution.py:64
  165.1 2.8 %fusion.127 = f32[8,512,2,128]{3,1,2,0:T(8,128)} fusion(f32[8,512,2,128]{3,1,2,0:T(8,128)} %get-tuple-element.853, s32[]{:T(128)} %get-tuple-element.851, bf16[512,2,128]{2,0,1:T(8,128)(2,1)S(1)} %get-tuple-element.874, f32[2,512,512]{1,2,0:T(8,128)S(1)} %get-tuple-element.751, f32[2,512]{1,0:T(2,128)S(1)} %get-tuple-element.753, ...), kind=kOutput, calls=%fused_computation.71.clone.1 | convolution fusion | flops 137101312 | bytes 3678720 | tf_op jit(solution)/shard_map/while/body/eval_jaxpr/kqc,ckd->qkd/dot_general | solution.py:64
  169.5 2.9 %fusion.127 = f32[8,512,2,128]{3,1,2,0:T(8,128)} fusion(f32[8,512,2,128]{3,1,2,0:T(8,128)} %get-tuple-element.853, s32[]{:T(128)} %get-tuple-element.851, bf16[512,2,128]{2,0,1:T(8,128)(2,1)S(1)} %get-tuple-element.874, f32[2,512,512]{1,2,0:T(8,128)S(1)} %get-tuple-element.751, f32[2,512]{1,0:T(2,128)S(1)} %get-tuple-element.753, ...), kind=kOutput, calls=%fused_computation.71.clone.1 | convolution fusion | flops 137101312 | bytes 3678720 | tf_op jit(solution)/shard_map/while/body/eval_jaxpr/kqc,ckd->qkd/dot_general | solution.py:64
  173.8 2.8 %fusion.127 = f32[8,512,2,128]{3,1,2,0:T(8,128)} fusion(f32[8,512,2,128]{3,1,2,0:T(8,128)} %get-tuple-element.853, s32[]{:T(128)} %get-tuple-element.851, bf16[512,2,128]{2,0,1:T(8,128)(2,1)S(1)} %get-tuple-element.874, f32[2,512,512]{1,2,0:T(8,128)S(1)} %get-tuple-element.751, f32[2,512]{1,0:T(2,128)S(1)} %get-tuple-element.753, ...), kind=kOutput, calls=%fused_computation.71.clone.1 | convolution fusion | flops 137101312 | bytes 3678720 | tf_op jit(solution)/shard_map/while/body/eval_jaxpr/kqc,ckd->qkd/dot_general | solution.py:64
  178.2 2.8 %fusion.127 = f32[8,512,2,128]{3,1,2,0:T(8,128)} fusion(f32[8,512,2,128]{3,1,2,0:T(8,128)} %get-tuple-element.853, s32[]{:T(128)} %get-tuple-element.851, bf16[512,2,128]{2,0,1:T(8,128)(2,1)S(1)} %get-tuple-element.874, f32[2,512,512]{1,2,0:T(8,128)S(1)} %get-tuple-element.751, f32[2,512]{1,0:T(2,128)S(1)} %get-tuple-element.753, ...), kind=kOutput, calls=%fused_computation.71.clone.1 | convolution fusion | flops 137101312 | bytes 3678720 | tf_op jit(solution)/shard_map/while/body/eval_jaxpr/kqc,ckd->qkd/dot_general | solution.py:64
  181.6 2.9 %fusion.73 = bf16[512,2,8,128]{3,0,1,2:T(8,128)(2,1)S(1)} fusion(f32[8,512,2,128]{3,1,2,0:T(8,128)} %get-tuple-element.167, f32[8,512,2]{1,2,0:T(2,128)S(1)} %bitcast.213), kind=kLoop, calls=%fused_computation.96 | loop fusion | flops 2097152 | bytes 6324224 | tf_op jit(solution)/shard_map/convert_element_type | solution.py:89
  184.5 2.7 %copy.75 = bf16[512,2,8,128]{3,2,1,0:T(8,128)(2,1)} copy(bf16[512,2,8,128]{3,0,1,2:T(8,128)(2,1)S(1)} %fusion.73) | data formatting | bytes 4194304 | tf_op jit(solution)/shard_map/convert_element_type | solution.py:89
  187.1 2.8 %convert_element_type.34 = bf16[4,128,2048]{2,1,0:T(8,128)(2,1)S(1)} reshape(bf16[512,2,8,128]{3,2,1,0:T(8,128)(2,1)} %copy.75) | data formatting | bytes 4194304 | tf_op jit(solution)/shard_map/convert_element_type | solution.py:89
  190.0 51.0 %all_to_all.64 = bf16[4,128,2048]{2,1,0:T(8,128)(2,1)} all-to-all(bf16[4,128,2048]{2,1,0:T(8,128)(2,1)S(1)} %convert_element_type.34), channel_id=1, replica_groups=mesh['head'=4,'outer'=2,'inner'=4] {'head'}, dimensions={0} | all-to-all | bytes 4194304 | tf_op jit(solution)/shard_map/all_to_all | solution.py:90
  241.0 3.0 %copy.76 = bf16[128,4,2048]{0,2,1:T(8,128)(2,1)S(1)} copy(bf16[128,4,2048]{2,0,1:T(8,128)(2,1)} %bitcast.202) | data formatting | bytes 4194304 | tf_op jit(solution)/shard_map/all_to_all | solution.py:90
  244.0 2.9 %copy.77 = bf16[128,8192]{1,0:T(8,128)(2,1)} copy(bf16[128,8192]{0,1:T(8,128)(2,1)S(1)} %bitcast.203) | data formatting | bytes 4194304 | tf_op jit(solution)/shard_map/all_to_all | solution.py:90
  (174 shorter events, 44.0 us)
Async XLA Ops:
  0.0 20.6 %copy-start = (bf16[128,8192]{1,0:T(8,128)(2,1)S(1)}, bf16[128,8192]{1,0:T(8,128)(2,1)}, u32[]{:S(2)}) copy-start(bf16[128,8192]{1,0:T(8,128)(2,1)} %param.10) | copy-start | bytes 6291460
  1.9 15.3 %all-to-all-start.1 = ((bf16[128,4,256]{0,2,1:T(8,128)(2,1)}), bf16[128,4,256]{0,2,1:T(8,128)(2,1)S(1)}, u32[]{:S(2)}, u32[]{:S(2)}) async-start(bf16[128,4,256]{0,2,1:T(8,128)(2,1)} %bitcast.2), calls=%async_computation.1 | async-start | bytes 524288 | tf_op jit(solution)/shard_map/all_to_all | solution.py:26
  17.2 10.4 %all-to-all-start.2 = ((bf16[128,4,256]{0,2,1:T(8,128)(2,1)}), bf16[128,4,256]{0,2,1:T(8,128)(2,1)S(1)}, u32[]{:S(2)}, u32[]{:S(2)}) async-start(bf16[128,4,256]{0,2,1:T(8,128)(2,1)} %bitcast.4), calls=%async_computation.2 | async-start | bytes 524288 | tf_op jit(solution)/shard_map/all_to_all | solution.py:27
  27.6 49.0 %all-to-all-start = ((bf16[128,4,2048]{2,0,1:T(8,128)(2,1)}), bf16[128,4,2048]{2,0,1:T(8,128)(2,1)S(1)}, u32[]{:S(2)}, u32[]{:S(2)}) async-start(bf16[128,4,2048]{2,0,1:T(8,128)(2,1)} %bitcast.143), calls=%async_computation | async-start | bytes 4194304 | tf_op jit(solution)/shard_map/all_to_all | solution.py:25
  31.2 17.2 %copy-start.3 = (s32[8]{0:T(128)S(1)}, s32[8]{0:T(128)}, u32[]{:S(2)}) copy-start(s32[8]{0:T(128)} %param.13) | copy-start | bytes 100
  31.6 11.6 %collective-permute-start = (bf16[2,512,256]{2,1,0:T(8,128)(2,1)S(1)}, bf16[2,512,256]{2,1,0:T(8,128)(2,1)}, u32[]{:S(2)}, u32[]{:S(2)}) collective-permute-start(bf16[2,512,256]{2,1,0:T(8,128)(2,1)S(1)} %pad_maximum_fusion), channel_id=1, source_target_pairs={{0,1},{1,2},{2,3},{3,4},{4,5},{5,6},{6,7},{8,9},{9,10},{10,11},{11... | collective-permute-start | bytes 1572872 | tf_op jit(solution)/shard_map/ppermute | solution.py:13
  43.2 13.9 %collective-permute-start.1 = (bf16[2,512,256]{2,1,0:T(8,128)(2,1)}, bf16[2,512,256]{2,1,0:T(8,128)(2,1)}, u32[]{:S(2)}, u32[]{:S(2)}) collective-permute-start(bf16[2,512,256]{2,1,0:T(8,128)(2,1)} %collective-permute-done), channel_id=1, source_target_pairs={{0,1},{1,2},{2,3},{3,4},{4,5},{5,6},{6,7},{8,9},{9,10},{10,11},{11... | collective-permute-start | bytes 1572872 | tf_op jit(solution)/shard_map/ppermute | solution.py:13
  80.5 1.0 copy-start.2
  83.8 1.0 copy-start.2
  87.2 1.0 copy-start.2
  90.5 1.0 copy-start.2
  93.9 1.0 copy-start.2
  97.2 1.0 copy-start.2
  100.6 1.0 copy-start.2
  103.9 1.0 copy-start.2
  107.2 2.4 copy-start.1
where the time goes:
time: 249 us; the launch traced here: 247 us
  matrix products  73 us (29%)
  blocking collectives  51 us (20%)
  waiting for transfers between devices  42.7 us (17%)
  local copies, waits for them, and re-layouts  30.7 us (12%)
  other arithmetic  25.2 us (10%)
  starting transfers between devices  22.9 us (9%)
    dot_general x24, matrix products, one_group(): jnp.einsum('kqc,ckd->qkd', weights.astype(jnp.bfloat16), value_heads, pre...  59.7 us
    all_to_all x1, blocking collectives, per_device(): lax.all_to_all(outcome, 'head', split_axis=0, concat_axis=1, tiled=True)  51 us
    all_to_all x1, waiting for transfers between devices, per_device(): lax.all_to_all(query, 'head', split_axis=1, concat_axis=0, tiled=True)  17.9 us
    reduce_sum x24, other arithmetic, one_group(): new_total = running_total * shrink + jnp.sum(weights, axis=2)  13.5 us
    dot_general x24, matrix products, one_group(): jnp.einsum('qkd,ckd->kqc', query_part, key_heads, preferred_element_type=...  13.3 us
    ppermute x2, waiting for transfers between devices, from_behind(): lax.ppermute(value, axis, [(source, source + steps) for source in range(l...  12.3 us
    ppermute x2, starting transfers between devices, from_behind(): lax.ppermute(value, axis, [(source, source + steps) for source in range(l...  9.49 us
    and x24, other arithmetic, attend(): (query_docs[:, None] == key_docs[None, :]) & (key_pos[None, :] <= query_p...  7.46 us
  transfers between devices with their start and end apart: 5, of which 5 were waited for; matrix products, arithmetic and copies ran while one was open for 4% of the time, Pallas kernels for 0%

commit v1 on v0

--- a/solution.py
+++ b/solution.py
@@ -87,7 +87,10 @@
     outcome = running_sum / jnp.transpose(running_total, (0, 2, 1))[..., None]
     outcome = jnp.transpose(outcome, (1, 2, 0, 3))
     outcome = outcome.reshape(local_len, pair_heads * group_width * HEAD_SIZE).astype(jnp.bfloat16)
-    return lax.all_to_all(outcome, "head", split_axis=0, concat_axis=1, tiled=True)
+    return jnp.concatenate(
+        lax.all_to_all(jnp.stack(jnp.split(outcome, lax.axis_size("head"), axis=0)), "head", 0, 0),
+        axis=1,
+    )
 
 
 def solution(mesh):

time: 249 us -> 269 us (1.080)
  matrix products: 73 us -> 89.4 us
  waiting for transfers between devices: 42.7 us -> 47.3 us
    dot_general x24, matrix products: 13.3 us -> 36 us  [one_group(): jnp.einsum('qkd,ckd->kqc', query_part, key_heads, preferred_element_type=...]
    dynamic_update_slice x0 -> x16, local copies, waits for them, and re-layouts: none -> 8.38 us  [attend(): return lax.map(one_group, (query_groups, state[0], state[1], state[2]))]
    dot_general x24, matrix products: 59.7 us -> 53.3 us  [one_group(): jnp.einsum('kqc,ckd->qkd', weights.astype(jnp.bfloat16), value_heads, pre...]
    all_to_all x2 -> x0, local copies, waits for them, and re-layouts: 5.92 us -> none  [per_device(): lax.all_to_all(outcome, 'head', split_axis=0, concat_axis=1, tiled=True)]
    convert_element_type x2 -> x0, local copies, waits for them, and re-layouts: 5.49 us -> none  [per_device(): outcome.reshape(local_len, pair_heads * group_width * HEAD_SIZE)]
    ppermute x2, waiting for transfers between devices: 12.3 us -> 16.1 us  [from_behind(): lax.ppermute(value, axis, [(source, source + steps) for source in range(l...]
    reshape x0 -> x1, local copies, waits for them, and re-layouts: none -> 2.88 us  [per_device(): jnp.concatenate(lax.all_to_all(jnp.stack(jnp.split(outcome, lax.axis_size...]
    another operation x8 -> x7, local copies, waits for them, and re-layouts: 7.23 us -> 4.87 us
  transfers between devices with their start and end apart: 5 -> 5, of which waited for: 5 -> 5; matrix products, arithmetic and copies ran while one was open for 4% -> 2% of each run, Pallas kernels for 0% -> 0%
where the time goes in v1:
time: 269 us; the launch traced here: 267 us
  matrix products  89.4 us (33%)
  blocking collectives  50.2 us (19%)
  waiting for transfers between devices  47.3 us (18%)
  local copies, waits for them, and re-layouts  31.4 us (12%)
  other arithmetic  25.4 us (9%)
  starting transfers between devices  22 us (8%)
    dot_general x24, matrix products, one_group(): jnp.einsum('kqc,ckd->qkd', weights.astype(jnp.bfloat16), value_heads, pre...  53.3 us
    all_to_all x1, blocking collectives, per_device(): lax.all_to_all(jnp.stack(jnp.split(outcome, lax.axis_size('head'), axis=0...  50.2 us
    dot_general x24, matrix products, one_group(): jnp.einsum('qkd,ckd->kqc', query_part, key_heads, preferred_element_type=...  36 us
    all_to_all x1, waiting for transfers between devices, per_device(): lax.all_to_all(query, 'head', split_axis=1, concat_axis=0, tiled=True)  18.5 us
    ppermute x2, waiting for transfers between devices, from_behind(): lax.ppermute(value, axis, [(source, source + steps) for source in range(l...  16.1 us
    reduce_sum x24, other arithmetic, one_group(): new_total = running_total * shrink + jnp.sum(weights, axis=2)  13.6 us
    unnamed x14, local copies, waits for them, and re-layouts  9.22 us
    dynamic_update_slice x16, local copies, waits for them, and re-layouts, attend(): return lax.map(one_group, (query_groups, state[0], state[1], state[2]))  8.38 us
  transfers between devices with their start and end apart: 5, of which 5 were waited for; matrix products, arithmetic and copies ran while one was open for 2% of the time, Pallas kernels for 0%

profile of v1, /device:TPU:0, one launch (start us, length us, event | category | flops | bytes accessed | tf_op | source)
XLA Modules:
  0.0 267.0 jit_solution(10690218235816409125)
XLA Ops:
  0.0 1.9 copy.58
  1.9 6.3 %all-to-all-start.1 = ((bf16[128,4,256]{0,2,1:T(8,128)(2,1)}), bf16[128,4,256]{0,2,1:T(8,128)(2,1)S(1)}, u32[]{:S(2)}, u32[]{:S(2)}) async-start(bf16[128,4,256]{0,2,1:T(8,128)(2,1)} %bitcast.2), calls=%async_computation.1 | async-start | bytes 524288 | tf_op jit(solution)/shard_map/all_to_all | solution.py:26
  8.3 1.8 copy.60
  10.1 7.1 %all-to-all-done.1 = bf16[128,4,256]{0,2,1:T(8,128)(2,1)S(1)} async-done(((bf16[128,4,256]{0,2,1:T(8,128)(2,1)}), bf16[128,4,256]{0,2,1:T(8,128)(2,1)S(1)}, u32[]{:S(2)}, u32[]{:S(2)}) %all-to-all-start.1) | async-done | bytes 262176 | tf_op jit(solution)/shard_map/all_to_all | solution.py:26
  17.2 3.4 %all-to-all-start.2 = ((bf16[128,4,256]{0,2,1:T(8,128)(2,1)}), bf16[128,4,256]{0,2,1:T(8,128)(2,1)S(1)}, u32[]{:S(2)}, u32[]{:S(2)}) async-start(bf16[128,4,256]{0,2,1:T(8,128)(2,1)} %bitcast.4), calls=%async_computation.2 | async-start | bytes 524288 | tf_op jit(solution)/shard_map/all_to_all | solution.py:27
  22.1 5.5 %all-to-all-done.2 = bf16[128,4,256]{0,2,1:T(8,128)(2,1)S(1)} async-done(((bf16[128,4,256]{0,2,1:T(8,128)(2,1)}), bf16[128,4,256]{0,2,1:T(8,128)(2,1)S(1)}, u32[]{:S(2)}, u32[]{:S(2)}) %all-to-all-start.2) | async-done | bytes 262176 | tf_op jit(solution)/shard_map/all_to_all | solution.py:27
  27.6 4.4 %all-to-all-start = ((bf16[128,4,2048]{2,0,1:T(8,128)(2,1)}), bf16[128,4,2048]{2,0,1:T(8,128)(2,1)}, u32[]{:S(2)}, u32[]{:S(2)}) async-start(bf16[128,4,2048]{2,0,1:T(8,128)(2,1)} %bitcast.142), calls=%async_computation | async-start | bytes 4194304 | tf_op jit(solution)/shard_map/all_to_all | solution.py:25
  32.4 3.4 %collective-permute-start = (bf16[2,512,256]{2,1,0:T(8,128)(2,1)S(1)}, bf16[2,512,256]{2,1,0:T(8,128)(2,1)S(1)}, u32[]{:S(2)}, u32[]{:S(2)}) collective-permute-start(bf16[2,512,256]{2,1,0:T(8,128)(2,1)S(1)} %pad_maximum_fusion.1), channel_id=1, source_target_pairs={{0,1},{1,2},{2,3},{3,4},{4,5},{5,6},{6,7},{8,9},{9,10},{10,11},{11... | collective-permute-start | bytes 1572872 | tf_op jit(solution)/shard_map/ppermute | solution.py:13
  35.9 8.1 %collective-permute-done = bf16[2,512,256]{2,1,0:T(8,128)(2,1)S(1)} collective-permute-done((bf16[2,512,256]{2,1,0:T(8,128)(2,1)S(1)}, bf16[2,512,256]{2,1,0:T(8,128)(2,1)S(1)}, u32[]{:S(2)}, u32[]{:S(2)}) %collective-permute-start) | collective-permute-done | bytes 524320 | tf_op jit(solution)/shard_map/ppermute | solution.py:13
  44.0 4.4 %collective-permute-start.1 = (bf16[2,512,256]{2,1,0:T(8,128)(2,1)S(1)}, bf16[2,512,256]{2,1,0:T(8,128)(2,1)S(1)}, u32[]{:S(2)}, u32[]{:S(2)}) collective-permute-start(bf16[2,512,256]{2,1,0:T(8,128)(2,1)S(1)} %collective-permute-done), channel_id=1, source_target_pairs={{0,1},{1,2},{2,3},{3,4},{4,5},{5,6},{6,7},{8,9},{9,10},{10,11},{11... | collective-permute-start | bytes 1572872 | tf_op jit(solution)/shard_map/ppermute | solution.py:13
  49.7 8.0 %collective-permute-done.1 = bf16[2,512,256]{2,1,0:T(8,128)(2,1)S(1)} collective-permute-done((bf16[2,512,256]{2,1,0:T(8,128)(2,1)S(1)}, bf16[2,512,256]{2,1,0:T(8,128)(2,1)S(1)}, u32[]{:S(2)}, u32[]{:S(2)}) %collective-permute-start.1) | collective-permute-done | bytes 524320 | tf_op jit(solution)/shard_map/ppermute | solution.py:13
  59.1 18.5 %all-to-all-done = bf16[128,4,2048]{2,0,1:T(8,128)(2,1)} async-done(((bf16[128,4,2048]{2,0,1:T(8,128)(2,1)}), bf16[128,4,2048]{2,0,1:T(8,128)(2,1)}, u32[]{:S(2)}, u32[]{:S(2)}) %all-to-all-start) | async-done | bytes 2097184 | tf_op jit(solution)/shard_map/all_to_all | solution.py:25
  77.6 2.2 copy.86
  79.8 1.9 copy.62
  81.7 2.4 broadcast.125.clone.1
  84.1 34.1 %while.43 = (s32[]{:T(128)}, f32[8,2,512]{2,1,0:T(2,128)S(1)}, f32[8,2,512]{2,1,0:T(2,128)S(1)}, f32[8,512,2,128]{3,1,2,0:T(8,128)}, bf16[8,512,2,128]{3,1,2,0:T...) while((s32[]{:T(128)}, f32[8,2,512]{2,1,0:T(2,128)S(1)}, ...), condition=%wide.region_5.6_spmd.clone, body=%wide.region_2.0_spmd.clone.sunk | while | flops 276435968 | bytes 8705649 | solution.py:73
  84.4 1.5 fusion.108
  86.0 1.8 fusion.111
  90.3 1.9 fusion.111
  94.6 1.8 fusion.111
  98.8 1.8 fusion.111
  103.0 1.8 fusion.111
  105.8 1.5 fusion.108
  107.3 1.8 fusion.111
  111.6 1.8 fusion.111
  115.8 1.8 fusion.111
  118.2 2.4 broadcast.125
  120.6 42.4 %while.44 = (s32[]{:T(128)}, f32[8,2,512]{2,1,0:T(2,128)S(1)}, f32[8,2,512]{2,1,0:T(2,128)S(1)}, f32[8,512,2,128]{3,1,2,0:T(8,128)}, f32[8,2,512]{2,1,0:T(2,128)...) while((s32[]{:T(128)}, f32[8,2,512]{2,1,0:T(2,128)S(1)}, ...), condition=%wide.region_10.11_spmd.clone, body=%wide.region_7.10_spmd.clone.sunk | while | flops 276566016 | bytes 9246365 | solution.py:73
  122.5 2.8 %fusion.119 = f32[8,512,2,128]{3,1,2,0:T(8,128)} fusion(f32[8,512,2,128]{3,1,2,0:T(8,128)} %get-tuple-element.811, s32[]{:T(128)} %get-tuple-element.808, bf16[512,2,128]{2,0,1:T(8,128)(2,1)S(1)} %get-tuple-element.833, f32[2,512,512]{1,2,0:T(8,128)S(1)} %get-tuple-element.735, f32[2,512]{1,0:T(2,128)S(1)} %get-tuple-element.737, ...), kind=kOutput, calls=%fused_computation.40.clone.1 | convolution fusion | flops 137101312 | bytes 3678720 | tf_op jit(solution)/shard_map/while/body/eval_jaxpr/kqc,ckd->qkd/dot_general | solution.py:64
  127.8 2.9 %fusion.119 = f32[8,512,2,128]{3,1,2,0:T(8,128)} fusion(f32[8,512,2,128]{3,1,2,0:T(8,128)} %get-tuple-element.811, s32[]{:T(128)} %get-tuple-element.808, bf16[512,2,128]{2,0,1:T(8,128)(2,1)S(1)} %get-tuple-element.833, f32[2,512,512]{1,2,0:T(8,128)S(1)} %get-tuple-element.735, f32[2,512]{1,0:T(2,128)S(1)} %get-tuple-element.737, ...), kind=kOutput, calls=%fused_computation.40.clone.1 | convolution fusion | flops 137101312 | bytes 3678720 | tf_op jit(solution)/shard_map/while/body/eval_jaxpr/kqc,ckd->qkd/dot_general | solution.py:64
  133.1 2.8 %fusion.119 = f32[8,512,2,128]{3,1,2,0:T(8,128)} fusion(f32[8,512,2,128]{3,1,2,0:T(8,128)} %get-tuple-element.811, s32[]{:T(128)} %get-tuple-element.808, bf16[512,2,128]{2,0,1:T(8,128)(2,1)S(1)} %get-tuple-element.833, f32[2,512,512]{1,2,0:T(8,128)S(1)} %get-tuple-element.735, f32[2,512]{1,0:T(2,128)S(1)} %get-tuple-element.737, ...), kind=kOutput, calls=%fused_computation.40.clone.1 | convolution fusion | flops 137101312 | bytes 3678720 | tf_op jit(solution)/shard_map/while/body/eval_jaxpr/kqc,ckd->qkd/dot_general | solution.py:64
  138.4 2.8 %fusion.119 = f32[8,512,2,128]{3,1,2,0:T(8,128)} fusion(f32[8,512,2,128]{3,1,2,0:T(8,128)} %get-tuple-element.811, s32[]{:T(128)} %get-tuple-element.808, bf16[512,2,128]{2,0,1:T(8,128)(2,1)S(1)} %get-tuple-element.833, f32[2,512,512]{1,2,0:T(8,128)S(1)} %get-tuple-element.735, f32[2,512]{1,0:T(2,128)S(1)} %get-tuple-element.737, ...), kind=kOutput, calls=%fused_computation.40.clone.1 | convolution fusion | flops 137101312 | bytes 3678720 | tf_op jit(solution)/shard_map/while/body/eval_jaxpr/kqc,ckd->qkd/dot_general | solution.py:64
  143.7 2.8 %fusion.119 = f32[8,512,2,128]{3,1,2,0:T(8,128)} fusion(f32[8,512,2,128]{3,1,2,0:T(8,128)} %get-tuple-element.811, s32[]{:T(128)} %get-tuple-element.808, bf16[512,2,128]{2,0,1:T(8,128)(2,1)S(1)} %get-tuple-element.833, f32[2,512,512]{1,2,0:T(8,128)S(1)} %get-tuple-element.735, f32[2,512]{1,0:T(2,128)S(1)} %get-tuple-element.737, ...), kind=kOutput, calls=%fused_computation.40.clone.1 | convolution fusion | flops 137101312 | bytes 3678720 | tf_op jit(solution)/shard_map/while/body/eval_jaxpr/kqc,ckd->qkd/dot_general | solution.py:64
  149.0 2.9 %fusion.119 = f32[8,512,2,128]{3,1,2,0:T(8,128)} fusion(f32[8,512,2,128]{3,1,2,0:T(8,128)} %get-tuple-element.811, s32[]{:T(128)} %get-tuple-element.808, bf16[512,2,128]{2,0,1:T(8,128)(2,1)S(1)} %get-tuple-element.833, f32[2,512,512]{1,2,0:T(8,128)S(1)} %get-tuple-element.735, f32[2,512]{1,0:T(2,128)S(1)} %get-tuple-element.737, ...), kind=kOutput, calls=%fused_computation.40.clone.1 | convolution fusion | flops 137101312 | bytes 3678720 | tf_op jit(solution)/shard_map/while/body/eval_jaxpr/kqc,ckd->qkd/dot_general | solution.py:64
  154.3 2.8 %fusion.119 = f32[8,512,2,128]{3,1,2,0:T(8,128)} fusion(f32[8,512,2,128]{3,1,2,0:T(8,128)} %get-tuple-element.811, s32[]{:T(128)} %get-tuple-element.808, bf16[512,2,128]{2,0,1:T(8,128)(2,1)S(1)} %get-tuple-element.833, f32[2,512,512]{1,2,0:T(8,128)S(1)} %get-tuple-element.735, f32[2,512]{1,0:T(2,128)S(1)} %get-tuple-element.737, ...), kind=kOutput, calls=%fused_computation.40.clone.1 | convolution fusion | flops 137101312 | bytes 3678720 | tf_op jit(solution)/shard_map/while/body/eval_jaxpr/kqc,ckd->qkd/dot_general | solution.py:64
  159.6 2.8 %fusion.119 = f32[8,512,2,128]{3,1,2,0:T(8,128)} fusion(f32[8,512,2,128]{3,1,2,0:T(8,128)} %get-tuple-element.811, s32[]{:T(128)} %get-tuple-element.808, bf16[512,2,128]{2,0,1:T(8,128)(2,1)S(1)} %get-tuple-element.833, f32[2,512,512]{1,2,0:T(8,128)S(1)} %get-tuple-element.735, f32[2,512]{1,0:T(2,128)S(1)} %get-tuple-element.737, ...), kind=kOutput, calls=%fused_computation.40.clone.1 | convolution fusion | flops 137101312 | bytes 3678720 | tf_op jit(solution)/shard_map/while/body/eval_jaxpr/kqc,ckd->qkd/dot_general | solution.py:64
  163.1 47.2 %while.45 = (s32[]{:T(128)}, f32[8,2,512]{2,1,0:T(2,128)S(1)}, f32[8,512,2,128]{1,3,0,2:T(8,128)}, f32[8,2,512]{2,1,0:T(2,128)S(1)}, f32[8,2,512]{2,1,0:T(2,128)...) while((s32[]{:T(128)}, f32[8,2,512]{2,1,0:T(2,128)S(1)}, ...), condition=%wide.region_15.16_spmd.clone, body=%wide.region_12.15_spmd.clone.sunk | while | flops 276566016 | bytes 14485229 | solution.py:73
  165.0 2.0 fusion.127
  170.9 2.0 fusion.127
  176.8 2.0 fusion.127
  182.7 2.0 fusion.127
  188.6 2.0 fusion.127
  194.4 2.0 fusion.127
  200.3 2.0 fusion.127
  206.2 2.0 fusion.127
  210.3 2.8 %fusion.72 = bf16[512,2,8,128]{0,3,2,1:T(8,128)(2,1)S(1)} fusion(f32[8,512,2,128]{1,3,0,2:T(8,128)} %get-tuple-element.167, f32[8,512,2]{1,0,2:T(8,128)S(1)} %copy.77), kind=kLoop, calls=%fused_computation.97 | loop fusion | flops 2097152 | bytes 6324224 | tf_op jit(solution)/shard_map/convert_element_type | solution.py:89
  214.0 50.2 %all_to_all.53 = bf16[4,128,2048]{1,2,0:T(8,128)(2,1)S(1)} all-to-all(bf16[4,128,2048]{1,2,0:T(8,128)(2,1)S(1)} %pad_maximum_fusion), channel_id=1, replica_groups=mesh['head'=4,'outer'=2,'inner'=4] {'head'}, dimensions={0} | all-to-all | bytes 4194304 | tf_op jit(solution)/shard_map/all_to_all | solution.py:91
  264.2 2.9 %copy.79 = bf16[128,8192]{1,0:T(8,128)(2,1)} copy(bf16[128,8192]{0,1:T(8,128)(2,1)S(1)} %bitcast.200) | data formatting | bytes 4194304 | tf_op jit(solution)/shard_map/reshape | solution.py:90
  (220 shorter events, 71.5 us)
Async XLA Ops:
  0.0 20.6 %copy-start.2 = (bf16[128,8192]{1,0:T(8,128)(2,1)S(1)}, bf16[128,8192]{1,0:T(8,128)(2,1)}, u32[]{:S(2)}) copy-start(bf16[128,8192]{1,0:T(8,128)(2,1)} %param.10) | copy-start | bytes 6291460
  1.9 15.3 %all-to-all-start.1 = ((bf16[128,4,256]{0,2,1:T(8,128)(2,1)}), bf16[128,4,256]{0,2,1:T(8,128)(2,1)S(1)}, u32[]{:S(2)}, u32[]{:S(2)}) async-start(bf16[128,4,256]{0,2,1:T(8,128)(2,1)} %bitcast.2), calls=%async_computation.1 | async-start | bytes 524288 | tf_op jit(solution)/shard_map/all_to_all | solution.py:26
  17.2 10.4 %all-to-all-start.2 = ((bf16[128,4,256]{0,2,1:T(8,128)(2,1)}), bf16[128,4,256]{0,2,1:T(8,128)(2,1)S(1)}, u32[]{:S(2)}, u32[]{:S(2)}) async-start(bf16[128,4,256]{0,2,1:T(8,128)(2,1)} %bitcast.4), calls=%async_computation.2 | async-start | bytes 524288 | tf_op jit(solution)/shard_map/all_to_all | solution.py:27
  27.6 50.0 %all-to-all-start = ((bf16[128,4,2048]{2,0,1:T(8,128)(2,1)}), bf16[128,4,2048]{2,0,1:T(8,128)(2,1)}, u32[]{:S(2)}, u32[]{:S(2)}) async-start(bf16[128,4,2048]{2,0,1:T(8,128)(2,1)} %bitcast.142), calls=%async_computation | async-start | bytes 4194304 | tf_op jit(solution)/shard_map/all_to_all | solution.py:25
  32.1 16.4 %copy-start.4 = (s32[8]{0:T(128)S(1)}, s32[8]{0:T(128)}, u32[]{:S(2)}) copy-start(s32[8]{0:T(128)} %param.13) | copy-start | bytes 100
  32.4 11.6 %collective-permute-start = (bf16[2,512,256]{2,1,0:T(8,128)(2,1)S(1)}, bf16[2,512,256]{2,1,0:T(8,128)(2,1)S(1)}, u32[]{:S(2)}, u32[]{:S(2)}) collective-permute-start(bf16[2,512,256]{2,1,0:T(8,128)(2,1)S(1)} %pad_maximum_fusion.1), channel_id=1, source_target_pairs={{0,1},{1,2},{2,3},{3,4},{4,5},{5,6},{6,7},{8,9},{9,10},{10,11},{11... | collective-permute-start | bytes 1572872 | tf_op jit(solution)/shard_map/ppermute | solution.py:13
  44.0 13.7 %collective-permute-start.1 = (bf16[2,512,256]{2,1,0:T(8,128)(2,1)S(1)}, bf16[2,512,256]{2,1,0:T(8,128)(2,1)S(1)}, u32[]{:S(2)}, u32[]{:S(2)}) collective-permute-start(bf16[2,512,256]{2,1,0:T(8,128)(2,1)S(1)} %collective-permute-done), channel_id=1, source_target_pairs={{0,1},{1,2},{2,3},{3,4},{4,5},{5,6},{6,7},{8,9},{9,10},{10,11},{11... | collective-permute-start | bytes 1572872 | tf_op jit(solution)/shard_map/ppermute | solution.py:13
  163.1 1.9 copy-start
  163.1 1.9 copy-start.3
  168.0 0.9 copy-start.1
  169.0 1.9 copy-start
  169.0 1.9 copy-start.3
  173.9 0.9 copy-start.1
  174.9 1.9 copy-start
  174.9 1.9 copy-start.3
  179.8 0.9 copy-start.1
  180.8 1.9 copy-start
  180.8 1.9 copy-start.3
  185.7 0.9 copy-start.1
  186.7 1.9 copy-start
  186.7 1.9 copy-start.3
  191.6 0.9 copy-start.1
  192.6 1.9 copy-start
  192.6 1.9 copy-start.3
  197.5 0.9 copy-start.1
  198.5 1.9 copy-start
  198.5 1.9 copy-start.3
  203.4 0.9 copy-start.1
  204.4 1.9 copy-start
  204.4 1.9 copy-start.3
  209.3 0.9 copy-start.1
